TPU v7x, 32 devices: a whole 2x2x4 slice. The times are simulated.
32 devices in a mesh: dp: 8 (over z, y), tp: 4 (over x, core).
Axes of the slice: x: 2, y: 2, z: 4, core: 2. Of those that a mesh axis runs over, the one named last changes fastest.
Arguments:
- tokens: bfloat16 [768, 2880], P('dp', 'tp'), may hold values from -100 to 100
- attn_gain: float32 [2880], replicated, may hold values from 0.1 to 1.9
- w_query: bfloat16 [2880, 2048], P(None, 'tp'), may hold values from -0.109375 to 0.109375
- w_keyvalue: bfloat16 [2880, 8, 128], P(None, 'tp'), may hold values from -0.109375 to 0.109375
- attn_sinks: float32 [32], P('tp'), may hold values from 2 to 6
- w_out: bfloat16 [2048, 2880], P('tp'), may hold values from -0.125 to 0.125
- window_cache: bfloat16 [768, 8, 128, 128], P('dp', 'tp'), may hold values from -1000 to 1000
- positions: int32 [768], P('dp'), may hold values from 0 to 511
- moe_gain: float32 [2880], replicated, may hold values from 0.1 to 1.9
- router: bfloat16 [2880, 8], P('tp'), may hold values from -0.109375 to 0.109375
- gate_up: bfloat16 [8, 2880, 2, 2880], P('dp', None, None, 'tp'), may hold values from -0.109375 to 0.109375
- w_down: bfloat16 [8, 2880, 2880], P('dp', None, 'tp'), may hold values from -0.109375 to 0.109375
- expert_ids: int32 [768, 4], P('dp'), may hold values from 0 to 7, all different within a row; in each aligned block of 96 rows (0 to 95, 96 to 191, ...) at most 96 rows name the same one
Outputs:
- layer_out: float32 [768, 2880], P('dp', 'tp')
Inputs may be any that keep to these rules, and one draw needn't show every extreme that they name: `expert_ids`: each row names 4 different experts. Within the rows of one index of dp no expert is named by more than 96 rows, a bound that some of these blocks reach.
All inputs are finite; a program needn't handle non-finite values.
Results may differ from a plain program's by a relative error of at most 0.0066.
Values may be sent and summed in bfloat16 or wider, within the bound.
A program may use at most 128 MiB of HBM per device.

v0:
```python
import jax
import jax.numpy as jnp
from jax import lax
from jax.sharding import PartitionSpec as P

norm_eps = 1e-05
rope_base = 150000.0
glu_alpha = 1.702


def rope_tables(positions, head_size):
    half_size = head_size // 2
    exponent = jnp.arange(half_size, dtype=jnp.float32) * (2.0 / head_size)
    inverse = jnp.power(jnp.float32(rope_base), -exponent)
    angles = positions.astype(jnp.float32)[:, None] * inverse[None, :]
    return (jnp.cos(angles), jnp.sin(angles))


def rotate(values, cosine, sine_table):
    half_size = values.shape[-1] // 2
    first_half = values[..., :half_size]
    second_half = values[..., half_size:]
    return jnp.concatenate(
        [
            first_half * cosine - second_half * sine_table,
            second_half * cosine + first_half * sine_table,
        ],
        axis=-1,
    )


def on_device(
    tokens,
    attn_gain,
    w_query,
    w_keyvalue,
    attn_sinks,
    w_out,
    window_cache,
    positions,
    moe_gain,
    router,
    gate_up,
    w_down,
    expert_ids,
):
    tp_count = lax.axis_size("tp")
    dp_count = lax.axis_size("dp")
    seq_count, col_count = tokens.shape
    full_width = col_count * tp_count
    col_start = lax.axis_index("tp") * col_count
    head_size = w_keyvalue.shape[2] // 2
    kv_local = w_keyvalue.shape[1]
    q_local = w_query.shape[1] // head_size
    group_size = q_local // kv_local
    window = window_cache.shape[2]
    attn_slice = lax.dynamic_slice_in_dim(attn_gain, col_start, col_count)
    moe_slice = lax.dynamic_slice_in_dim(moe_gain, col_start, col_count)
    tok_wide = tokens.astype(jnp.float32)
    attn_sq = lax.psum(jnp.sum(tok_wide * tok_wide, axis=1), "tp")
    normed = (
        tok_wide * lax.rsqrt(attn_sq / full_width + norm_eps)[:, None] * attn_slice[None, :]
    ).astype(jnp.bfloat16)
    kv_flat = w_keyvalue.reshape(full_width, kv_local * 2 * head_size)
    piece_rows = lax.all_gather(normed, "tp", axis=1, tiled=True)
    queries = jnp.dot(piece_rows, w_query, preferred_element_type=jnp.float32)
    fresh_rows = jnp.dot(piece_rows, kv_flat, preferred_element_type=jnp.float32)
    cosine, sine_table = rope_tables(positions, head_size)
    rot_queries = rotate(
        queries.reshape(seq_count, q_local, head_size), cosine[:, None, :], sine_table[:, None, :]
    ).astype(jnp.bfloat16)
    fresh_rows = fresh_rows.reshape(seq_count, kv_local, 2 * head_size)
    new_key = rotate(fresh_rows[..., :head_size], cosine[:, None, :], sine_table[:, None, :])
    new_entry = jnp.concatenate([new_key, fresh_rows[..., head_size:]], axis=-1).astype(
        jnp.bfloat16
    )
    slot_ids = jnp.arange(window, dtype=jnp.int32)
    is_current = slot_ids[None, :] == (positions % window)[:, None]
    cache_now = jnp.where(is_current[:, None, :, None], new_entry[:, :, None, :], window_cache)
    is_valid = (positions[:, None] - slot_ids[None, :]) % window <= positions[:, None]
    grouped = rot_queries.reshape(seq_count, kv_local, group_size, head_size)
    scores = jnp.einsum(
        "skgh,skwh->skgw", grouped, cache_now[..., :head_size], preferred_element_type=jnp.float32
    ) * head_size ** (-0.5)
    scores = jnp.where(is_valid[:, None, None, :], scores, -jnp.inf)
    sink_col = attn_sinks.reshape(kv_local, group_size)[None, :, :, None]
    peak_score = jnp.maximum(jnp.max(scores, axis=-1, keepdims=True), sink_col)
    raised = jnp.exp(scores - peak_score)
    denominator = jnp.sum(raised, axis=-1, keepdims=True) + jnp.exp(sink_col - peak_score)
    prob_bf = (raised / denominator).astype(jnp.bfloat16)
    attended = jnp.einsum(
        "skgw,skwh->skgh", prob_bf, cache_now[..., head_size:], preferred_element_type=jnp.float32
    ).astype(jnp.bfloat16)
    partial_out = jnp.dot(
        attended.reshape(seq_count, q_local * head_size), w_out, preferred_element_type=jnp.float32
    )
    residual = tok_wide + lax.psum_scatter(
        partial_out.astype(jnp.bfloat16), "tp", scatter_dimension=1, tiled=True
    ).astype(jnp.float32)
    experts = router.shape[1]
    top_count = expert_ids.shape[1]
    local_experts = gate_up.shape[0]
    ff_local = gate_up.shape[3]
    capacity = min(seq_count, max(2, 8 * seq_count * top_count // (3 * experts)))
    moe_sq = jnp.sum(residual * residual, axis=1)
    router_wide = router.astype(jnp.float32)
    total_sq = lax.psum(moe_sq, "tp")
    moe_scale = lax.rsqrt(total_sq / full_width + norm_eps)[:, None]
    scaled = residual * moe_scale * moe_slice[None, :]
    logits = lax.psum(jnp.dot(scaled, router_wide, precision=lax.Precision.HIGHEST), "tp")
    hidden_rows = scaled.astype(jnp.bfloat16)
    expert_iota = jnp.arange(experts, dtype=jnp.int32)
    chosen = expert_ids[:, :, None] == expert_iota[None, None, :]
    picked = jnp.sum(jnp.where(chosen, logits[:, None, :], 0.0), axis=-1)
    raised_logits = jnp.exp(picked)
    route_weights = raised_logits / jnp.sum(raised_logits, axis=1, keepdims=True)
    assign = expert_ids.reshape(-1)
    onehot = (assign[:, None] == expert_iota[None, :]).astype(jnp.int32)
    earlier = jnp.cumsum(onehot, axis=0) - onehot
    slot_of = jnp.sum(earlier * onehot, axis=1)
    target = (assign * capacity + slot_of).reshape(seq_count, top_count)
    spot_ids = jnp.arange(experts * capacity, dtype=jnp.int32)
    slot_hits = target[:, :, None] == spot_ids[None, None, :]
    placer = jnp.transpose(jnp.any(slot_hits, axis=1)).astype(jnp.bfloat16)
    combiner = jnp.sum(jnp.where(slot_hits, route_weights[:, :, None], 0.0), axis=1)
    gate_up_flat = gate_up.reshape(local_experts, full_width, 2 * ff_local)
    placed = jnp.dot(placer, hidden_rows, preferred_element_type=jnp.float32).astype(jnp.bfloat16)
    mixed_in = jnp.einsum(
        "gecd,edf->gecf",
        lax.all_gather(
            lax.all_to_all(
                placed.reshape(dp_count, local_experts, capacity, hidden_rows.shape[1]),
                "dp",
                split_axis=0,
                concat_axis=0,
                tiled=True,
            ),
            "tp",
            axis=3,
            tiled=True,
        ),
        gate_up_flat,
        preferred_element_type=jnp.float32,
    )
    gate_part = mixed_in[..., :ff_local]
    up_part = mixed_in[..., ff_local:]
    act_rows = (gate_part * jax.nn.sigmoid(glu_alpha * gate_part) * (up_part + 1.0)).astype(
        jnp.bfloat16
    )
    answered = jnp.einsum(
        "gecf,efd->gecd",
        lax.all_gather(act_rows, "tp", axis=3, tiled=True),
        w_down,
        preferred_element_type=jnp.float32,
    ).astype(jnp.bfloat16)
    returned = lax.all_to_all(answered, "dp", split_axis=0, concat_axis=0, tiled=True)
    flat_back = returned.reshape(experts * capacity, col_count).astype(jnp.float32)
    moe_out = jnp.dot(combiner, flat_back, precision=lax.Precision.HIGHEST)
    return residual + moe_out


def solution(mesh):
    in_specs = (
        P("dp", "tp"),
        P(),
        P(None, "tp"),
        P(None, "tp", None),
        P("tp"),
        P("tp", None),
        P("dp", "tp", None, None),
        P("dp"),
        P(),
        P("tp", None),
        P("dp", None, None, "tp"),
        P("dp", None, "tp"),
        P("dp", None),
    )
    out_specs = P("dp", "tp")
    return jax.shard_map(
        on_device, mesh=mesh, in_specs=in_specs, out_specs=out_specs, check_vma=False
    )
```

profile of v0, /device:TPU:0, one launch (start us, length us, event | category | flops | bytes accessed | tf_op | source)
XLA Modules:
  0.0 306.0 jit_solution(1373459359515891442)
XLA Ops:
  6.6 1.2 fusion.37
  7.8 8.4 %psum.21 = f32[96]{0:T(128)S(1)} all-reduce(f32[96]{0:T(128)S(1)} %fusion.37), channel_id=1, replica_groups=mesh['dp'=8,'tp'=4] {'tp'}, use_global_device_ids=true, to_apply=%region_1.0 | all-reduce | flops 96 | bytes 768 | tf_op jit(solution)/shard_map/psum | solution.py:60
  16.1 0.8 dynamic_slice.6
  16.9 1.0 fusion.48
  17.9 6.7 %all-gather = bf16[4,720,96]{1,2,0:T(8,128)(2,1)S(1)} all-gather(bf16[1,720,96]{1,2,0:T(8,128)(2,1)S(1)} %fusion.48), channel_id=1, replica_groups=mesh['dp'=8,'tp'=4] {'tp'}, dimensions={0}, use_global_device_ids=true | all-gather | bytes 691200 | tf_op jit(solution)/shard_map/all_gather | solution.py:65
  24.6 0.5 copy.86
  25.1 1.3 reshape.248
  26.4 1.3 reshape.247
  27.6 0.5 fusion.63
  28.2 0.7 fusion.54
  28.9 4.9 %copy.111 = bf16[2880,2,128]{0,2,1:T(8,128)(2,1)} copy(bf16[2880,2,128]{2,1,0:T(2,128)(2,1)} %param.16) | data formatting | bytes 2949120 | tf_op jit(solution)/shard_map/dot_general | solution.py:67
  33.7 0.1 multiply_cosine_fusion
  33.9 0.7 copy.92
  34.6 0.7 copy.93
  35.3 2.0 fusion.19
  37.3 0.1 slice.84
  37.4 0.9 subtract_convert_fusion.1
  38.3 0.1 pad_maximum_fusion
  38.4 0.7 copy.94
  39.1 1.3 iota_compare_fusion.1
  40.4 8.7 %copy.95 = bf16[96,2,128,128]{2,3,1,0:T(8,128)(2,1)} copy(bf16[96,2,128,128]{3,2,1,0:T(8,128)(2,1)} %param.19) | data formatting | bytes 12582912 | tf_op args[6]
  49.1 3.1 %fusion.65 = f32[96,512]{0,1:T(8,128)S(1)} fusion(bf16[2880,96]{0,1:T(8,128)(2,1)S(1)} %copy-done.3, bf16[2880,512]{1,0:T(8,128)(2,1)} %param.15), kind=kOutput, calls=%fused_computation.91 | convolution fusion | flops 283115520 | bytes 3698688 | tf_op jit(solution)/shard_map/dot_general | solution.py:66
  52.3 0.2 copy.88
  52.4 0.2 copy.89
  52.6 0.1 max.18
  52.7 7.2 %broadcast_select_fusion = bf16[96,2,128,128]{2,3,1,0:T(8,128)(2,1)S(1)} fusion(bf16[96,2,128,128]{2,3,1,0:T(8,128)(2,1)} %copy.95, pred[96,128]{1,0:T(8,128)(4,1)} %iota_compare_fusion.1, bf16[96,2,128]{2,1,0:T(2,128)(2,1)} %copy.94), kind=kLoop, calls=%fused_computation | loop fusion | flops 3145728 | bytes 12644352 | tf_op jit(solution)/shard_map/jit(_where)/select_n | solution.py:79
  59.9 1.2 fusion.64
  61.2 0.6 fusion.36
  61.8 1.8 fusion.33
  63.6 0.2 copy.96
  63.8 1.9 convolution_convert_fusion
  65.7 2.2 copy.112
  68.0 0.1 copy.97
  68.1 0.1 eq.76
  68.2 0.1 eq.72
  68.3 0.8 dynamic_slice.7
  69.1 0.8 reduce-window.6
  69.9 0.2 slice_reduce_fusion
  70.2 0.1 fusion.59
  70.3 0.1 reduce_sum.68
  70.5 0.2 fusion.32
  70.7 21.4 %reduce-scatter.4.cloned.1.call-done = bf16[720,96]{1,0:T(8,128)(2,1)} async-done(((bf16[2880,96]{1,0:T(8,128)(2,1)}), bf16[720,96]{1,0:T(8,128)(2,1)}) %reduce-scatter.4.cloned.1.call-update) | async-done | bytes 138256
  92.1 1.0 copy.113
  93.2 0.1 multiply_reduce_fusion
  93.3 5.8 %psum.22 = f32[96]{0:T(128)S(1)} all-reduce(f32[96]{0:T(128)S(1)} %multiply_reduce_fusion), channel_id=1, replica_groups=mesh['dp'=8,'tp'=4] {'tp'}, use_global_device_ids=true, to_apply=%region_9.10 | all-reduce | flops 96 | bytes 768 | tf_op jit(solution)/shard_map/psum | solution.py:107
  99.1 0.6 convolution_convert_fusion.1
  99.7 0.6 copy.100
  100.3 34.2 %all_to_all.10 = bf16[8,1,96,720]{3,2,1,0:T(8,128)(2,1)S(1)} all-to-all(bf16[8,1,96,720]{3,2,1,0:T(8,128)(2,1)S(1)} %bitcast.88), channel_id=1, replica_groups=mesh['dp'=8,'tp'=4] {'dp'}, dimensions={0} | all-to-all | bytes 2211840 | tf_op jit(solution)/shard_map/all_to_all | solution.py:131
  134.5 1.9 copy.102
  136.5 0.2 all-gather.6.cloned.1.call-start
  136.7 41.8 %all-gather.4.cloned.1.call-done = bf16[8,1,96,2880]{2,0,1,3:T(8,128)(2,1)} async-done(((bf16[8,1,96,720]{2,0,1,3:T(8,128)(2,1)}), bf16[8,1,96,2880]{2,0,1,3:T(8,128)(2,1)}) %all-gather.4.cloned.1.call-update) | async-done | bytes 4423696 | tf_op jit(solution)/shard_map/all_gather | solution.py:130
  178.5 8.3 %copy.103 = bf16[8,1,96,2880]{3,2,0,1:T(8,128)(2,1)} copy(bf16[8,1,96,2880]{2,0,1,3:T(8,128)(2,1)} %all-gather.4.cloned.1.call-done) | data formatting | bytes 8847360 | tf_op jit(solution)/shard_map/all_gather | solution.py:130
  186.8 11.4 %fusion.5 = f32[8,1,96,1440]{3,2,0,1:T(8,128)S(1)} fusion(bf16[2880,1440,1]{0,1,2:T(8,128)(2,1)} %bitcast.104, bf16[8,1,96,2880]{3,2,0,1:T(8,128)(2,1)} %copy.103), kind=kOutput, calls=%fused_computation.6 | convolution fusion | flops 6370099200 | bytes 17141760 | tf_op jit(solution)/shard_map/gecd,edf->gecf/dot_general | solution.py:128
  198.2 0.8 fusion.13
  199.1 1.9 copy.104
  201.0 44.3 %all-gather.6.cloned.1.call-done = bf16[8,1,96,2880]{2,0,1,3:T(8,128)(2,1)} async-done(((bf16[8,1,96,720]{2,0,1,3:T(8,128)(2,1)}), bf16[8,1,96,2880]{2,0,1,3:T(8,128)(2,1)}) %all-gather.6.cloned.1.call-update) | async-done | bytes 4423696 | tf_op jit(solution)/shard_map/all_gather | solution.py:152
  245.3 8.3 %copy.105 = bf16[8,1,96,2880]{3,2,0,1:T(8,128)(2,1)} copy(bf16[8,1,96,2880]{2,0,1,3:T(8,128)(2,1)} %all-gather.6.cloned.1.call-done) | data formatting | bytes 8847360 | tf_op jit(solution)/shard_map/all_gather | solution.py:152
  253.6 8.6 %fusion.21 = bf16[8,1,96,720]{3,2,1,0:T(8,128)(2,1)} fusion(bf16[1,2880,720]{1,2,0:T(8,128)(2,1)} %param.24, bf16[8,1,96,2880]{3,2,0,1:T(8,128)(2,1)} %copy.105), kind=kOutput, calls=%fused_computation.19 | convolution fusion | flops 3185602560 | bytes 9676800 | tf_op jit(solution)/shard_map/gecf,efd->gecd/dot_general | solution.py:150
  262.2 5.5 %all-to-all-start.1 = ((bf16[8,1,96,720]{3,2,1,0:T(8,128)(2,1)}), bf16[8,1,96,720]{3,2,1,0:T(8,128)(2,1)}, u32[]{:S(2)}, u32[]{:S(2)}) async-start(bf16[8,1,96,720]{3,2,1,0:T(8,128)(2,1)} %fusion.21), calls=%async_computation.1 | async-start | bytes 2359296 | tf_op jit(solution)/shard_map/all_to_all | solution.py:156
  267.7 0.3 fusion.41
  268.0 6.2 %psum.23 = f32[96,8]{0,1:T(8,128)S(1)} all-reduce(f32[96,8]{0,1:T(8,128)S(1)} %fusion.41), channel_id=1, replica_groups=mesh['dp'=8,'tp'=4] {'tp'}, use_global_device_ids=true, to_apply=%region_10.11 | all-reduce | flops 768 | bytes 6144 | tf_op jit(solution)/shard_map/psum | solution.py:110
  274.3 0.2 select_reduce_fusion
  274.5 22.3 %all-to-all-done.1 = bf16[8,1,96,720]{3,2,1,0:T(8,128)(2,1)} async-done(((bf16[8,1,96,720]{3,2,1,0:T(8,128)(2,1)}), bf16[8,1,96,720]{3,2,1,0:T(8,128)(2,1)}, u32[]{:S(2)}, u32[]{:S(2)}) %all-to-all-start.1) | async-done | bytes 1105952 | tf_op jit(solution)/shard_map/all_to_all | solution.py:156
  296.8 2.7 convolution_add_fusion
  (40 shorter events, 0.4 us)
Async XLA Ops:
  6.5 57.3 %copy-start = (bf16[512,2880]{0,1:T(8,128)(2,1)S(1)}, bf16[512,2880]{0,1:T(8,128)(2,1)}, u32[]{:S(2)}) copy-start(bf16[512,2880]{0,1:T(8,128)(2,1)} %param.18) | copy-start | bytes 8847364
  6.5 21.1 %copy-start.7 = (s32[96]{0:T(128)S(1)}, s32[96]{0:T(128)}, u32[]{:S(2)}) copy-start(s32[96]{0:T(128)} %param.20) | copy-start | bytes 1156
  6.5 85.6 %reduce-scatter.4.cloned.1.call-start = ((), (), s32[]{:S(2)}) async-start(), calls=%async_computation.5 | async-start | bytes 921600
  27.6 7.7 %copy-start.4 = (bf16[2880,96,1]{0,1,2:T(8,128)(2,1)S(1)}, bf16[2880,96,1]{0,1,2:T(8,128)(2,1)}, u32[]{:S(2)}) copy-start(bf16[2880,96,1]{0,1,2:T(8,128)(2,1)} %reshape.248) | copy-start | bytes 1658884
  40.4 8.7 %copy-start.3 = (bf16[2880,96]{0,1:T(8,128)(2,1)S(1)}, bf16[2880,96]{0,1:T(8,128)(2,1)}, u32[]{:S(2)}) copy-start(bf16[2880,96]{0,1:T(8,128)(2,1)} %reshape.247) | copy-start | bytes 1658884
  49.1 3.5 %copy-start.9 = (f32[8]{0:T(128)S(1)}, f32[8]{0:T(128)}, u32[]{:S(2)}) copy-start(f32[8]{0:T(128)} %param.17) | copy-start | bytes 100
  52.7 7.2 %copy-start.6 = (pred[96,128]{1,0:T(8,128)(4,1)S(1)}, pred[96,128]{1,0:T(8,128)(4,1)}, u32[]{:S(2)}) copy-start(pred[96,128]{1,0:T(8,128)(4,1)} %fusion.54) | copy-start | bytes 36868
  63.6 4.4 %copy-start.5 = (s32[96,4]{0,1:T(4,128)S(1)}, s32[96,4]{0,1:T(4,128)}, u32[]{:S(2)}) copy-start(s32[96,4]{0,1:T(4,128)} %param.25) | copy-start | bytes 4612
  63.8 29.4 %copy-start.2 = (bf16[96,720]{1,0:T(8,128)(2,1)S(1)}, bf16[96,720]{1,0:T(8,128)(2,1)}, u32[]{:S(2)}) copy-start(bf16[96,720]{1,0:T(8,128)(2,1)} %param.13) | copy-start | bytes 414724
  67.9 110.5 %all-gather.4.cloned.1.call-start = ((), (), s32[]{:S(2)}) async-start(), calls=%async_computation.3 | async-start | bytes 7372800 | tf_op jit(solution)/shard_map/all_gather | solution.py:130
  136.5 108.8 %all-gather.6.cloned.1.call-start = ((), (), s32[]{:S(2)}) async-start(), calls=%async_computation.4 | async-start | bytes 7372800 | tf_op jit(solution)/shard_map/all_gather | solution.py:152
  253.6 14.1 %copy-start.8 = (bf16[720,8]{0,1:T(8,128)(2,1)S(1)}, bf16[720,8]{0,1:T(8,128)(2,1)}, u32[]{:S(2)}) copy-start(bf16[720,8]{0,1:T(8,128)(2,1)} %param.22) | copy-start | bytes 34564
  253.6 45.9 %copy-start.1 = (bf16[512,2880]{0,1:T(8,128)(2,1)S(1)}, bf16[512,2880]{0,1:T(8,128)(2,1)}, u32[]{:S(2)}) copy-start(bf16[512,2880]{0,1:T(8,128)(2,1)} %param.18) | copy-start | bytes 8847364
  262.2 34.6 %all-to-all-start.1 = ((bf16[8,1,96,720]{3,2,1,0:T(8,128)(2,1)}), bf16[8,1,96,720]{3,2,1,0:T(8,128)(2,1)}, u32[]{:S(2)}, u32[]{:S(2)}) async-start(bf16[8,1,96,720]{3,2,1,0:T(8,128)(2,1)} %fusion.21), calls=%async_computation.1 | async-start | bytes 2359296 | tf_op jit(solution)/shard_map/all_to_all | solution.py:156
Sparse Core Ops, SparseCore 0:
  68.0 24.0 reduce-scatter.3
  136.6 41.8 all-gather.3
  201.1 44.1 all-gather.5
where the time goes:
time: 307 us; the launch traced here: 306 us
  waiting for transfers between devices  130 us (42%)
  blocking collectives  61.2 us (20%)
  local copies, waits for them, and re-layouts  46.1 us (15%)
  matrix products  33.5 us (11%)
  other arithmetic  16.2 us (5%)
  between operations  13.4 us (4%)
  starting transfers between devices  5.78 us (2%)
    all_gather x1, waiting for transfers between devices, on_device(): lax.all_gather(act_rows, 'tp', axis=3, tiled=True)  44.3 us
    all_gather x1, waiting for transfers between devices, on_device(): lax.all_gather(lax.all_to_all(placed.reshape(dp_count, local_experts, cap...  41.8 us
    all_to_all x1, blocking collectives, on_device(): lax.all_to_all(placed.reshape(dp_count, local_experts, capacity, hidden_r...  34.2 us
    all_to_all x1, waiting for transfers between devices, on_device(): lax.all_to_all(answered, 'dp', split_axis=0, concat_axis=0, tiled=True)  22.3 us
    unnamed x4, waiting for transfers between devices  21.5 us
    unnamed x28, local copies, waits for them, and re-layouts  14.7 us
    dot_general x1, matrix products, on_device(): jnp.einsum('gecd,edf->gecf', lax.all_gather(lax.all_to_all(placed.reshape...  11.4 us
    dot_general x1, matrix products, on_device(): jnp.einsum('gecf,efd->gecd', lax.all_gather(act_rows, 'tp', axis=3, tiled...  8.57 us
  transfers between devices with their start and end apart: 4, of which 4 were waited for; matrix products, arithmetic and copies ran while one was open for 1% of the time, Pallas kernels for 0%

commit v1 on v0

--- a/solution.py
+++ b/solution.py
@@ -6,6 +6,22 @@
 norm_eps = 1e-05
 rope_base = 150000.0
 glu_alpha = 1.702
+
+
+def product_in_turn(x, axis, dim, product):
+    length, here, width = (lax.axis_size(axis), lax.axis_index(axis), x.shape[dim])
+    right = [(i, (i + 1) % length) for i in range(length)]
+    behind = [(i, (i - 1) % length) for i in range(length)]
+    halfway = length // 2
+    from_left = from_right = x
+    running = product(x, here * width)
+    for hop in range(1, halfway + 1):
+        from_left = lax.ppermute(from_left, axis, right)
+        if hop < length - halfway:
+            from_right = lax.ppermute(from_right, axis, behind)
+            running = running + product(from_right, (here + hop) % length * width)
+        running = running + product(from_left, (here - hop) % length * width)
+    return running
 
 
 def rope_tables(positions, head_size):
@@ -147,11 +163,16 @@
     act_rows = (gate_part * jax.nn.sigmoid(glu_alpha * gate_part) * (up_part + 1.0)).astype(
         jnp.bfloat16
     )
-    answered = jnp.einsum(
-        "gecf,efd->gecd",
-        lax.all_gather(act_rows, "tp", axis=3, tiled=True),
-        w_down,
-        preferred_element_type=jnp.float32,
+    answered = product_in_turn(
+        act_rows,
+        "tp",
+        3,
+        lambda shard, start: jnp.einsum(
+            "gecf,efd->gecd",
+            shard,
+            lax.dynamic_slice_in_dim(w_down, start, shard.shape[3], axis=1),
+            preferred_element_type=jnp.float32,
+        ),
     ).astype(jnp.bfloat16)
     returned = lax.all_to_all(answered, "dp", split_axis=0, concat_axis=0, tiled=True)
     flat_back = returned.reshape(experts * capacity, col_count).astype(jnp.float32)

time: 307 us -> 289 us (0.941)
  waiting for transfers between devices: 130 us -> 117 us
  local copies, waits for them, and re-layouts: 46.1 us -> 35.8 us
  matrix products: 33.5 us -> 37 us
    all_gather x1 -> x0, waiting for transfers between devices: 44.3 us -> none  [on_device(): lax.all_gather(act_rows, 'tp', axis=3, tiled=True)]
    ppermute x0 -> x3, waiting for transfers between devices: none -> 33.7 us  [the longest x2 33.7 us: product_in_turn(): from_left = lax.ppermute(from_left, axis, right)]
    all_gather x1 -> x0, local copies, waits for them, and re-layouts: 8.35 us -> none  [on_device(): lax.all_gather(act_rows, 'tp', axis=3, tiled=True)]
    dot_general x1 -> x4, matrix products: 8.57 us -> 12 us  [on_device(): jnp.einsum('gecf,efd->gecd', shard, lax.dynamic_slice_in_dim(w_down, star...]
    unnamed x4 -> x3, waiting for transfers between devices: 21.5 us -> 21.4 us
  transfers between devices with their start and end apart: 4 -> 6, of which waited for: 4 -> 5; matrix products, arithmetic and copies ran while one was open for 1% -> 4% of each run, Pallas kernels for 0% -> 0%
where the time goes in v1:
time: 289 us; the launch traced here: 288 us
  waiting for transfers between devices  117 us (40%)
  blocking collectives  61.1 us (21%)
  matrix products  37 us (13%)
  local copies, waits for them, and re-layouts  35.8 us (12%)
  other arithmetic  16.2 us (6%)
  between operations  13.7 us (5%)
  starting transfers between devices  7.28 us (3%)
    all_gather x1, waiting for transfers between devices, on_device(): lax.all_gather(lax.all_to_all(placed.reshape(dp_count, local_experts, cap...  42 us
    all_to_all x1, blocking collectives, on_device(): lax.all_to_all(placed.reshape(dp_count, local_experts, capacity, hidden_r...  34.2 us
    ppermute x2, waiting for transfers between devices, product_in_turn(): from_left = lax.ppermute(from_left, axis, right)  33.7 us
    unnamed x3, waiting for transfers between devices  21.4 us
    all_to_all x1, waiting for transfers between devices, on_device(): lax.all_to_all(answered, 'dp', split_axis=0, concat_axis=0, tiled=True)  19.6 us
    unnamed x28, local copies, waits for them, and re-layouts  14.7 us
    dot_general x4, matrix products, on_device(): jnp.einsum('gecf,efd->gecd', shard, lax.dynamic_slice_in_dim(w_down, star...  12 us
    dot_general x1, matrix products, on_device(): jnp.einsum('gecd,edf->gecf', lax.all_gather(lax.all_to_all(placed.reshape...  11.4 us
  transfers between devices with their start and end apart: 6, of which 5 were waited for; matrix products, arithmetic and copies ran while one was open for 4% of the time, Pallas kernels for 0%

profile of v1, /device:TPU:0, one launch (start us, length us, event | category | flops | bytes accessed | tf_op | source)
XLA Modules:
  0.0 287.8 jit_solution(7466907026957487872)
XLA Ops:
  6.6 1.2 fusion.40
  7.8 8.4 %psum.21 = f32[96]{0:T(128)S(1)} all-reduce(f32[96]{0:T(128)S(1)} %fusion.40), channel_id=1, replica_groups=mesh['dp'=8,'tp'=4] {'tp'}, use_global_device_ids=true, to_apply=%region_1.0 | all-reduce | flops 96 | bytes 768 | tf_op jit(solution)/shard_map/psum | solution.py:76
  16.1 0.8 dynamic_slice.18
  16.9 1.0 fusion.51
  17.9 6.7 %all-gather = bf16[4,720,96]{1,2,0:T(8,128)(2,1)S(1)} all-gather(bf16[1,720,96]{1,2,0:T(8,128)(2,1)S(1)} %fusion.51), channel_id=1, replica_groups=mesh['dp'=8,'tp'=4] {'tp'}, dimensions={0}, use_global_device_ids=true | all-gather | bytes 691200 | tf_op jit(solution)/shard_map/all_gather | solution.py:81
  24.6 0.5 copy.98
  25.1 1.3 reshape.278
  26.4 1.3 reshape.277
  27.6 0.5 fusion.70
  28.2 0.7 fusion.57
  28.9 4.9 %copy.125 = bf16[2880,2,128]{0,2,1:T(8,128)(2,1)} copy(bf16[2880,2,128]{2,1,0:T(2,128)(2,1)} %param.16) | data formatting | bytes 2949120 | tf_op jit(solution)/shard_map/dot_general | solution.py:83
  33.8 0.1 multiply_cosine_fusion
  33.9 0.7 copy.104
  34.6 0.7 copy.105
  35.3 2.0 fusion.11
  37.4 0.9 subtract_convert_fusion.1
  38.3 0.1 pad_maximum_fusion
  38.4 0.7 copy.106
  39.1 1.3 iota_compare_fusion.1
  40.4 8.7 %copy.107 = bf16[96,2,128,128]{2,3,1,0:T(8,128)(2,1)} copy(bf16[96,2,128,128]{3,2,1,0:T(8,128)(2,1)} %param.19) | data formatting | bytes 12582912 | tf_op args[6]
  49.1 3.1 %fusion.72 = f32[96,512]{0,1:T(8,128)S(1)} fusion(bf16[2880,96]{0,1:T(8,128)(2,1)S(1)} %copy-done.3, bf16[2880,512]{1,0:T(8,128)(2,1)} %param.15), kind=kOutput, calls=%fused_computation.107 | convolution fusion | flops 283115520 | bytes 3698688 | tf_op jit(solution)/shard_map/dot_general | solution.py:82
  52.3 0.2 copy.100
  52.4 0.2 copy.101
  52.7 7.2 %broadcast_select_fusion = bf16[96,2,128,128]{2,3,1,0:T(8,128)(2,1)S(1)} fusion(bf16[96,2,128,128]{2,3,1,0:T(8,128)(2,1)} %copy.107, pred[96,128]{1,0:T(8,128)(4,1)} %iota_compare_fusion.1, bf16[96,2,128]{2,1,0:T(2,128)(2,1)} %copy.106), kind=kLoop, calls=%fused_computation | loop fusion | flops 3145728 | bytes 12644352 | tf_op jit(solution)/shard_map/jit(_where)/select_n | solution.py:95
  59.9 1.2 fusion.71
  61.2 0.6 fusion.39
  61.8 1.8 fusion.28
  63.6 0.2 copy.108
  63.8 1.9 convolution_convert_fusion
  65.7 2.2 copy.126
  68.0 0.1 copy.109
  68.1 0.1 eq.80
  68.2 0.1 eq.76
  68.3 0.8 dynamic_slice.19
  69.1 0.8 reduce-window.6
  69.9 0.2 slice_reduce_fusion
  70.3 0.1 reduce_sum.68
  70.5 0.2 fusion.27
  70.7 21.4 %reduce-scatter.4.cloned.1.call-done = bf16[720,96]{1,0:T(8,128)(2,1)} async-done(((bf16[2880,96]{1,0:T(8,128)(2,1)}), bf16[720,96]{1,0:T(8,128)(2,1)}) %reduce-scatter.4.cloned.1.call-update) | async-done | bytes 138256
  92.2 1.0 copy.127
  93.2 0.1 multiply_reduce_fusion
  93.4 5.8 %psum.22 = f32[96]{0:T(128)S(1)} all-reduce(f32[96]{0:T(128)S(1)} %multiply_reduce_fusion), channel_id=1, replica_groups=mesh['dp'=8,'tp'=4] {'tp'}, use_global_device_ids=true, to_apply=%region_9.10 | all-reduce | flops 96 | bytes 768 | tf_op jit(solution)/shard_map/psum | solution.py:123
  99.1 0.6 convolution_convert_fusion.1
  99.7 0.6 copy.113
  100.4 34.2 %all_to_all.10 = bf16[8,1,96,720]{3,2,1,0:T(8,128)(2,1)S(1)} all-to-all(bf16[8,1,96,720]{3,2,1,0:T(8,128)(2,1)S(1)} %bitcast.103), channel_id=1, replica_groups=mesh['dp'=8,'tp'=4] {'dp'}, dimensions={0} | all-to-all | bytes 2211840 | tf_op jit(solution)/shard_map/all_to_all | solution.py:147
  134.6 1.9 copy.115
  136.5 42.0 %all-gather.3.cloned.1.call-done = bf16[8,1,96,2880]{2,0,1,3:T(8,128)(2,1)} async-done(((bf16[8,1,96,720]{2,0,1,3:T(8,128)(2,1)}), bf16[8,1,96,2880]{2,0,1,3:T(8,128)(2,1)}) %all-gather.3.cloned.1.call-update) | async-done | bytes 4423696 | tf_op jit(solution)/shard_map/all_gather | solution.py:146
  178.5 8.3 %copy.116 = bf16[8,1,96,2880]{3,2,0,1:T(8,128)(2,1)} copy(bf16[8,1,96,2880]{2,0,1,3:T(8,128)(2,1)} %all-gather.3.cloned.1.call-done) | data formatting | bytes 8847360 | tf_op jit(solution)/shard_map/all_gather | solution.py:146
  186.8 11.4 %fusion.2 = f32[8,1,96,1440]{3,2,0,1:T(8,128)S(1)} fusion(bf16[2880,1440,1]{0,1,2:T(8,128)(2,1)} %bitcast.119, bf16[8,1,96,2880]{3,2,0,1:T(8,128)(2,1)} %copy.116), kind=kOutput, calls=%fused_computation.3 | convolution fusion | flops 6370099200 | bytes 17141760 | tf_op jit(solution)/shard_map/gecd,edf->gecf/dot_general | solution.py:144
  198.2 0.8 fusion.10
  199.1 0.3 collective-permute-start.1
  199.4 1.5 collective-permute-start
  200.9 25.9 %collective-permute-done.1 = bf16[8,1,96,720]{3,2,0,1:T(8,128)(2,1)S(1)} collective-permute-done((bf16[8,1,96,720]{3,2,0,1:T(8,128)(2,1)S(1)}, bf16[8,1,96,720]{3,2,0,1:T(8,128)(2,1)S(1)}, u32[]{:S(2)}, u32[]{:S(2)}) %collective-permute-start.1) | collective-permute-done | bytes 1105952 | tf_op jit(solution)/shard_map/ppermute | solution.py:19
  226.8 2.5 fusion.25
  229.3 2.5 fusion.21
  231.8 2.9 fusion.23
  234.7 7.8 %collective-permute-done.2 = bf16[8,1,96,720]{3,2,0,1:T(8,128)(2,1)} collective-permute-done((bf16[8,1,96,720]{3,2,0,1:T(8,128)(2,1)S(1)}, bf16[8,1,96,720]{3,2,0,1:T(8,128)(2,1)}, u32[]{:S(2)}, u32[]{:S(2)}) %collective-permute-start.2) | collective-permute-done | bytes 1105952 | tf_op jit(solution)/shard_map/ppermute | solution.py:19
  242.5 4.1 %fusion.13 = bf16[8,1,96,720]{3,2,1,0:T(8,128)(2,1)} fusion(f32[720,8,96]{0,2,1:T(8,128)S(1)} %fusion.21, f32[720,8,96]{0,2,1:T(8,128)S(1)} %fusion.25, f32[720,8,96]{0,2,1:T(8,128)S(1)} %fusion.23, bf16[8,1,96,720]{3,2,0,1:T(8,128)(2,1)} %collective-permute-done.2, bf16[1,2880,720]{1,2,0:T(8,128)(2,1)} %param.24, s32[]{:T(128)S(6)} %select_n.73), kind=kOutput, calls=%fused_computation.16 | convolution fusion | flops 798474240 | bytes 10027012 | tf_op jit(solution)/shard_map/gecf,efd->gecd/dot_general | solution.py:170
  246.6 5.4 %all-to-all-start.1 = ((bf16[8,1,96,720]{3,2,1,0:T(8,128)(2,1)}), bf16[8,1,96,720]{3,2,1,0:T(8,128)(2,1)}, u32[]{:S(2)}, u32[]{:S(2)}) async-start(bf16[8,1,96,720]{3,2,1,0:T(8,128)(2,1)} %fusion.13), calls=%async_computation.1 | async-start | bytes 2359296 | tf_op jit(solution)/shard_map/all_to_all | solution.py:177
  252.1 0.3 fusion.44
  252.4 6.1 %psum.23 = f32[96,8]{0,1:T(8,128)S(1)} all-reduce(f32[96,8]{0,1:T(8,128)S(1)} %fusion.44), channel_id=1, replica_groups=mesh['dp'=8,'tp'=4] {'tp'}, use_global_device_ids=true, to_apply=%region_10.11 | all-reduce | flops 768 | bytes 6144 | tf_op jit(solution)/shard_map/psum | solution.py:126
  258.5 0.2 select_reduce_fusion
  258.7 19.6 %all-to-all-done.1 = bf16[8,1,96,720]{3,2,1,0:T(8,128)(2,1)} async-done(((bf16[8,1,96,720]{3,2,1,0:T(8,128)(2,1)}), bf16[8,1,96,720]{3,2,1,0:T(8,128)(2,1)}, u32[]{:S(2)}, u32[]{:S(2)}) %all-to-all-start.1) | async-done | bytes 1105952 | tf_op jit(solution)/shard_map/all_to_all | solution.py:177
  278.3 2.7 convolution_add_fusion
  (44 shorter events, 0.7 us)
Async XLA Ops:
  6.5 57.3 %copy-start = (bf16[512,2880]{0,1:T(8,128)(2,1)S(1)}, bf16[512,2880]{0,1:T(8,128)(2,1)}, u32[]{:S(2)}) copy-start(bf16[512,2880]{0,1:T(8,128)(2,1)} %param.18) | copy-start | bytes 8847364
  6.5 21.1 %copy-start.7 = (s32[96]{0:T(128)S(1)}, s32[96]{0:T(128)}, u32[]{:S(2)}) copy-start(s32[96]{0:T(128)} %param.20) | copy-start | bytes 1156
  6.5 85.6 %reduce-scatter.4.cloned.1.call-start = ((), (), s32[]{:S(2)}) async-start(), calls=%async_computation.4 | async-start | bytes 921600
  27.6 7.7 %copy-start.4 = (bf16[2880,96,1]{0,1,2:T(8,128)(2,1)S(1)}, bf16[2880,96,1]{0,1,2:T(8,128)(2,1)}, u32[]{:S(2)}) copy-start(bf16[2880,96,1]{0,1,2:T(8,128)(2,1)} %reshape.278) | copy-start | bytes 1658884
  40.4 8.7 %copy-start.3 = (bf16[2880,96]{0,1:T(8,128)(2,1)S(1)}, bf16[2880,96]{0,1:T(8,128)(2,1)}, u32[]{:S(2)}) copy-start(bf16[2880,96]{0,1:T(8,128)(2,1)} %reshape.277) | copy-start | bytes 1658884
  49.1 3.5 %copy-start.9 = (f32[8]{0:T(128)S(1)}, f32[8]{0:T(128)}, u32[]{:S(2)}) copy-start(f32[8]{0:T(128)} %param.17) | copy-start | bytes 100
  52.7 7.2 %copy-start.6 = (pred[96,128]{1,0:T(8,128)(4,1)S(1)}, pred[96,128]{1,0:T(8,128)(4,1)}, u32[]{:S(2)}) copy-start(pred[96,128]{1,0:T(8,128)(4,1)} %fusion.57) | copy-start | bytes 36868
  63.8 4.2 %copy-start.5 = (s32[96,4]{0,1:T(4,128)S(1)}, s32[96,4]{0,1:T(4,128)}, u32[]{:S(2)}) copy-start(s32[96,4]{0,1:T(4,128)} %param.25) | copy-start | bytes 4612
  63.8 29.4 %copy-start.2 = (bf16[96,720]{1,0:T(8,128)(2,1)S(1)}, bf16[96,720]{1,0:T(8,128)(2,1)}, u32[]{:S(2)}) copy-start(bf16[96,720]{1,0:T(8,128)(2,1)} %param.13) | copy-start | bytes 414724
  67.9 110.5 %all-gather.3.cloned.1.call-start = ((), (), s32[]{:S(2)}) async-start(), calls=%async_computation.3 | async-start | bytes 7372800 | tf_op jit(solution)/shard_map/all_gather | solution.py:146
  199.1 27.7 %collective-permute-start.1 = (bf16[8,1,96,720]{3,2,0,1:T(8,128)(2,1)S(1)}, bf16[8,1,96,720]{3,2,0,1:T(8,128)(2,1)S(1)}, u32[]{:S(2)}, u32[]{:S(2)}) collective-permute-start(bf16[8,1,96,720]{3,2,0,1:T(8,128)(2,1)S(1)} %fusion.10), channel_id=1, source_target_pairs={{0,1},{1,2},{2,3},{3,0},{4,5},{5,6},{6,7},{7,4},{8,9},{9,10},{10,1... | collective-permute-start | bytes 3317768 | tf_op jit(solution)/shard_map/ppermute | solution.py:19
  199.4 32.4 %collective-permute-start = (bf16[8,1,96,720]{3,2,0,1:T(8,128)(2,1)S(1)}, bf16[8,1,96,720]{3,2,0,1:T(8,128)(2,1)}, u32[]{:S(2)}, u32[]{:S(2)}) collective-permute-start(bf16[8,1,96,720]{3,2,0,1:T(8,128)(2,1)S(1)} %fusion.10), channel_id=1, source_target_pairs={{0,3},{1,0},{2,1},{3,2},{4,7},{5,4},{6,5},{7,6},{8,11},{9,8},{10,9... | collective-permute-start | bytes 3317768 | tf_op jit(solution)/shard_map/ppermute | solution.py:21
  226.8 15.7 %collective-permute-start.2 = (bf16[8,1,96,720]{3,2,0,1:T(8,128)(2,1)S(1)}, bf16[8,1,96,720]{3,2,0,1:T(8,128)(2,1)}, u32[]{:S(2)}, u32[]{:S(2)}) collective-permute-start(bf16[8,1,96,720]{3,2,0,1:T(8,128)(2,1)S(1)} %collective-permute-done.1), channel_id=1, source_target_pairs={{0,1},{1,2},{2,3},{3,0},{4,5},{5,6},{6,7},{7,4},{8,9},{9,10},{10,1... | collective-permute-start | bytes 3317768 | tf_op jit(solution)/shard_map/ppermute | solution.py:19
  242.5 38.5 %copy-start.1 = (bf16[512,2880]{0,1:T(8,128)(2,1)S(1)}, bf16[512,2880]{0,1:T(8,128)(2,1)}, u32[]{:S(2)}) copy-start(bf16[512,2880]{0,1:T(8,128)(2,1)} %param.18) | copy-start | bytes 8847364
  246.6 5.4 %copy-start.8 = (bf16[720,8]{0,1:T(8,128)(2,1)S(1)}, bf16[720,8]{0,1:T(8,128)(2,1)}, u32[]{:S(2)}) copy-start(bf16[720,8]{0,1:T(8,128)(2,1)} %param.22) | copy-start | bytes 34564
  246.6 31.7 %all-to-all-start.1 = ((bf16[8,1,96,720]{3,2,1,0:T(8,128)(2,1)}), bf16[8,1,96,720]{3,2,1,0:T(8,128)(2,1)}, u32[]{:S(2)}, u32[]{:S(2)}) async-start(bf16[8,1,96,720]{3,2,1,0:T(8,128)(2,1)} %fusion.13), calls=%async_computation.1 | async-start | bytes 2359296 | tf_op jit(solution)/shard_map/all_to_all | solution.py:177
Sparse Core Ops, SparseCore 0:
  68.0 24.0 reduce-scatter.3
  136.6 41.8 all-gather.2
